TPU v7x, 32 devices: a whole 2x2x4 slice. The times are simulated.
32 devices in a mesh: groups: 2 (over y), blk: 4 (over z), rep: 2 (over x), sub: 2 (over core).
Axes of the slice: x: 2, y: 2, z: 4, core: 2. Of those that a mesh axis runs over, the one named last changes fastest.
Arguments:
- replica_delta: bfloat16 [32, 32, 4608], P(('groups', 'blk', 'rep', 'sub')), parts along dimension 0, may hold values from -150 to 150
- momentum: float32 [64, 4608], P(('groups', 'blk')), parts along dimension 0, may hold values from -6 to 6
- params: float32 [64, 4608], P(('groups', 'blk')), parts along dimension 0, may hold values from -6 to 6
- prev_master: float32 [64, 4608], P(('groups', 'blk')), parts along dimension 0, may hold values from -6 to 6
Outputs:
- new_params: float32 [64, 4608], P(('groups', 'blk')), parts along dimension 0
- new_momentum: float32 [64, 4608], P(('groups', 'blk')), parts along dimension 0
- prev_weights: bfloat16 [64, 4608], P('groups'), parts along dimension 0
There are 2 independent parts, one for each index of `groups`. A program takes and returns all parts, laid end to end along the dimension named above; each array names one. Nothing has to cross between parts.
All inputs are finite; a program needn't handle non-finite values.
Results may differ from a plain program's by a relative error of at most 0.012.
Values may be sent and summed in bfloat16 or wider, within the bound.
No kernel may reach another device: no remote copies, remote signals or barrier semaphores. Data moves between devices by JAX's collectives and lax.ppermute only.
A program may use at most 64 MiB of HBM per device.

v0:
```python
import jax
import jax.numpy as jnp
from jax import lax
from jax.sharding import PartitionSpec as P

momentum_coef = 0.9
outer_rate = 0.7


def per_device(replica_delta, momentum, params, prev_master):
    own_delta = replica_delta[0]
    width = own_delta.shape[1]
    entries = own_delta.shape[0] * width
    share_sum = lax.psum_scatter(
        own_delta.astype(jnp.float32).astype(jnp.bfloat16), "blk", scatter_dimension=0, tiled=True
    )
    summed = lax.psum(share_sum, ("rep", "sub")).astype(jnp.float32)
    squares = lax.psum(jnp.sum(summed * summed), "blk")
    clip_factor = jnp.minimum(
        jnp.float32(1.0), jnp.sqrt(jnp.float32(entries)) / jnp.sqrt(squares + 1e-06)
    )
    scaled = clip_factor * summed
    new_momentum = momentum_coef * momentum + scaled
    new_params = params - outer_rate * (scaled + momentum_coef * new_momentum)
    prev_weights = lax.all_gather(prev_master.astype(jnp.bfloat16), "blk", axis=0, tiled=True)
    return (new_params, new_momentum, prev_weights)


def solution(mesh):
    in_specs = (
        P(("groups", "blk", "rep", "sub"), None, None),
        P(("groups", "blk"), None),
        P(("groups", "blk"), None),
        P(("groups", "blk"), None),
    )
    out_specs = (P(("groups", "blk"), None), P(("groups", "blk"), None), P("groups", None))
    return jax.shard_map(
        per_device, mesh=mesh, in_specs=in_specs, out_specs=out_specs, check_vma=False
    )
```

profile of v0, /device:TPU:0, one launch (start us, length us, event | category | flops | bytes accessed | tf_op | source)
XLA Modules:
  0.0 86.8 jit_solution(3447558341183904942)
XLA Ops:
  7.2 0.0 reduce-scatter.2.cloned.1.call-start
  7.2 0.0 copy-start.1
  7.2 0.7 reduce-scatter.2.cloned.1.call-update
  7.9 0.0 all-reduce.2.cloned.1.call-start
  7.9 0.2 copy-done.1
  8.1 25.1 %reduce-scatter.2.cloned.1.call-done = bf16[8,4608]{1,0:T(8,128)(2,1)} async-done(((bf16[32,4608]{1,0:T(8,128)(2,1)}), bf16[8,4608]{1,0:T(8,128)(2,1)}) %reduce-scatter.2.cloned.1.call-update) | async-done | bytes 73744 | tf_op jit(solution)/shard_map/reduce_scatter | solution.py:14
  33.2 0.0 all-reduce.2.cloned.1.call-update
  33.2 0.0 copy-start.2
  33.2 0.0 copy-start.3
  33.2 14.1 %all_gather.3 = bf16[32,4608]{1,0:T(8,128)(2,1)S(1)} all-gather(bf16[8,4608]{1,0:T(8,128)(2,1)S(1)} %convert_element_type.9), channel_id=1, replica_groups=mesh['groups'=2,'blk'=4,'rep'=2,'sub'=2] {'blk'}, dimensions={0}, use_global_device_ids=true | all-gather | bytes 368640 | tf_op jit(solution)/shard_map/all_gather | solution.py:25
  47.4 16.1 %all-reduce.2.cloned.1.call-done = bf16[8,4608]{1,0:T(8,128)(2,1)} async-done(((bf16[8,4608]{1,0:T(8,128)(2,1)}), bf16[8,4608]{1,0:T(8,128)(2,1)}) %all-reduce.2.cloned.1.call-update) | async-done | bytes 73744 | tf_op jit(solution)/shard_map/psum | solution.py:17
  63.5 0.0 copy-start
  63.5 1.6 %fusion.4 = f32[]{:T(128)} fusion(bf16[8,4608]{1,0:T(8,128)(2,1)} %all-reduce.2.cloned.1.call-done), kind=kLoop, calls=%fused_computation.6 | loop fusion | flops 110591 | bytes 73732 | tf_op jit(solution)/shard_map/reduce_sum | solution.py:18
  65.1 12.7 %psum.15 = f32[]{:T(128)} all-reduce(f32[]{:T(128)} %fusion.4), channel_id=1, replica_groups=mesh['groups'=2,'blk'=4,'rep'=2,'sub'=2] {'blk'}, use_global_device_ids=true, to_apply=%region_3.0 | all-reduce | flops 1 | bytes 8 | tf_op jit(solution)/shard_map/psum | solution.py:18
  78.4 0.0 copy-done.2
  78.5 0.0 copy-done.3
  78.5 0.0 copy-done
  78.5 0.8 fusion.3
  79.2 0.7 copy.9
  (1 shorter events, 0.0 us)
Async XLA Ops:
  7.2 26.0 %reduce-scatter.2.cloned.1.call-start = ((), (), s32[]{:S(2)}) async-start(), calls=%async_computation.1 | async-start | bytes 368640 | tf_op jit(solution)/shard_map/reduce_scatter | solution.py:14
  7.2 0.9 %copy-start.1 = (f32[8,4608]{1,0:T(8,128)S(1)}, f32[8,4608]{1,0:T(8,128)}, u32[]{:S(2)}) copy-start(f32[8,4608]{1,0:T(8,128)} %param.7) | copy-start | bytes 442372
  7.9 55.6 %all-reduce.2.cloned.1.call-start = ((), (), s32[]{:S(2)}) async-start(), calls=%async_computation.2 | async-start | bytes 147456 | tf_op jit(solution)/shard_map/psum | solution.py:17
  33.2 45.2 %copy-start.2 = (f32[8,4608]{1,0:T(8,128)S(1)}, f32[8,4608]{1,0:T(8,128)}, u32[]{:S(2)}) copy-start(f32[8,4608]{1,0:T(8,128)} %param.6) | copy-start | bytes 442372
  33.2 45.2 %copy-start.3 = (f32[8,4608]{1,0:T(8,128)S(1)}, f32[8,4608]{1,0:T(8,128)}, u32[]{:S(2)}) copy-start(f32[8,4608]{1,0:T(8,128)} %param.5) | copy-start | bytes 442372
  63.5 15.0 %copy-start = (bf16[8,4608]{1,0:T(8,128)(2,1)S(1)}, bf16[8,4608]{1,0:T(8,128)(2,1)}, u32[]{:S(2)}) copy-start(bf16[8,4608]{1,0:T(8,128)(2,1)} %all-reduce.2.cloned.1.call-done) | copy-start | bytes 221188
Sparse Core Ops, SparseCore 0:
  10.2 22.9 reduce-scatter.1
  35.5 27.9 all-reduce.1
where the time goes:
time: 87 us; the launch traced here: 86.8 us
  waiting for transfers between devices  41.9 us (48%)
  blocking collectives  26.8 us (31%)
  between operations  14.8 us (17%)
  other arithmetic  2.36 us (3%)
  local copies, waits for them, and re-layouts  0.91 us (1%)
    reduce_scatter x1, waiting for transfers between devices, per_device(): lax.psum_scatter(own_delta.astype(jnp.float32).astype(jnp.bfloat16), 'blk...  25.1 us
    psum x1, waiting for transfers between devices, per_device(): summed = lax.psum(share_sum, ('rep', 'sub')).astype(jnp.float32)  16.1 us
    all_gather x1, blocking collectives, per_device(): lax.all_gather(prev_master.astype(jnp.bfloat16), 'blk', axis=0, tiled=True)  14.1 us
    psum x1, blocking collectives, per_device(): squares = lax.psum(jnp.sum(summed * summed), 'blk')  12.7 us
  transfers between devices with their start and end apart: 2, of which 2 were waited for; matrix products, arithmetic and copies ran while one was open for 0% of the time, Pallas kernels for 0%

commit v1 on v0

--- a/solution.py
+++ b/solution.py
@@ -14,7 +14,7 @@
     share_sum = lax.psum_scatter(
         own_delta.astype(jnp.float32).astype(jnp.bfloat16), "blk", scatter_dimension=0, tiled=True
     )
-    summed = lax.psum(share_sum, ("rep", "sub")).astype(jnp.float32)
+    summed = lax.psum(lax.psum(share_sum, "sub"), "rep").astype(jnp.float32)
     squares = lax.psum(jnp.sum(summed * summed), "blk")
     clip_factor = jnp.minimum(
         jnp.float32(1.0), jnp.sqrt(jnp.float32(entries)) / jnp.sqrt(squares + 1e-06)

time: 87 us -> 98.8 us (1.14)
  waiting for transfers between devices: 41.9 us -> 53.9 us
    psum x1 -> x2, waiting for transfers between devices: 16.1 us -> 28 us  [per_device(): summed = lax.psum(lax.psum(share_sum, 'sub'), 'rep').astype(jnp.float32)]
  transfers between devices with their start and end apart: 2 -> 3, of which waited for: 2 -> 3; matrix products, arithmetic and copies ran while one was open for 0% -> 0% of each run, Pallas kernels for 0% -> 0%
where the time goes in v1:
time: 98.8 us; the launch traced here: 98.6 us
  waiting for transfers between devices  53.9 us (55%)
  blocking collectives  26.9 us (27%)
  between operations  14.5 us (15%)
  other arithmetic  2.36 us (2%)
    psum x2, waiting for transfers between devices, per_device(): summed = lax.psum(lax.psum(share_sum, 'sub'), 'rep').astype(jnp.float32)  28 us
    reduce_scatter x1, waiting for transfers between devices, per_device(): lax.psum_scatter(own_delta.astype(jnp.float32).astype(jnp.bfloat16), 'blk...  25.3 us
    all_gather x1, blocking collectives, per_device(): lax.all_gather(prev_master.astype(jnp.bfloat16), 'blk', axis=0, tiled=True)  14.6 us
    psum x1, blocking collectives, per_device(): squares = lax.psum(jnp.sum(summed * summed), 'blk')  12.3 us
  transfers between devices with their start and end apart: 3, of which 3 were waited for; matrix products, arithmetic and copies ran while one was open for 0% of the time, Pallas kernels for 0%

profile of v1, /device:TPU:0, one launch (start us, length us, event | category | flops | bytes accessed | tf_op | source)
XLA Modules:
  0.0 98.6 jit_solution(16130087390763525409)
XLA Ops:
  7.2 0.0 reduce-scatter.2.cloned.1.call-start
  7.2 0.0 copy-start.1
  7.2 0.7 reduce-scatter.2.cloned.1.call-update
  7.9 0.0 all-reduce.3.cloned.1.call-start
  7.9 25.3 %reduce-scatter.2.cloned.1.call-done = bf16[8,4608]{1,0:T(8,128)(2,1)} async-done(((bf16[32,4608]{1,0:T(8,128)(2,1)}), bf16[8,4608]{1,0:T(8,128)(2,1)}) %reduce-scatter.2.cloned.1.call-update) | async-done | bytes 73744 | tf_op jit(solution)/shard_map/reduce_scatter | solution.py:14
  33.2 0.0 all-reduce.3.cloned.1.call-update
  33.2 0.0 all-reduce.5.cloned.1.call-start
  33.3 0.0 copy-done.1
  33.3 18.2 %all-reduce.3.cloned.1.call-done = bf16[8,4608]{1,0:T(8,128)(2,1)} async-done(((bf16[8,4608]{1,0:T(8,128)(2,1)}), bf16[8,4608]{1,0:T(8,128)(2,1)}) %all-reduce.3.cloned.1.call-update) | async-done | bytes 73744 | tf_op jit(solution)/shard_map/psum | solution.py:17
  51.5 0.0 all-reduce.5.cloned.1.call-update
  51.5 0.0 copy-start.2
  51.5 0.0 copy-start.3
  51.5 14.6 %all_gather.3 = bf16[32,4608]{1,0:T(8,128)(2,1)S(1)} all-gather(bf16[8,4608]{1,0:T(8,128)(2,1)S(1)} %convert_element_type.9), channel_id=1, replica_groups=mesh['groups'=2,'blk'=4,'rep'=2,'sub'=2] {'blk'}, dimensions={0}, use_global_device_ids=true | all-gather | bytes 368640 | tf_op jit(solution)/shard_map/all_gather | solution.py:25
  66.1 9.8 %all-reduce.5.cloned.1.call-done = bf16[8,4608]{1,0:T(8,128)(2,1)} async-done(((bf16[8,4608]{1,0:T(8,128)(2,1)}), bf16[8,4608]{1,0:T(8,128)(2,1)}) %all-reduce.5.cloned.1.call-update) | async-done | bytes 73744 | tf_op jit(solution)/shard_map/psum | solution.py:17
  75.9 0.0 copy-start
  75.9 1.6 %fusion.4 = f32[]{:T(128)} fusion(bf16[8,4608]{1,0:T(8,128)(2,1)} %all-reduce.5.cloned.1.call-done), kind=kLoop, calls=%fused_computation.6 | loop fusion | flops 110591 | bytes 73732 | tf_op jit(solution)/shard_map/reduce_sum | solution.py:18
  77.5 12.3 %psum.23 = f32[]{:T(128)} all-reduce(f32[]{:T(128)} %fusion.4), channel_id=1, replica_groups=mesh['groups'=2,'blk'=4,'rep'=2,'sub'=2] {'blk'}, use_global_device_ids=true, to_apply=%region_4.0 | all-reduce | flops 1 | bytes 8 | tf_op jit(solution)/shard_map/psum | solution.py:18
  90.5 0.0 copy-done.2
  90.5 0.0 copy-done.3
  90.6 0.0 copy-done
  90.6 0.8 fusion.3
  91.3 0.7 copy.10
  (1 shorter events, 0.0 us)
Async XLA Ops:
  7.2 26.0 %reduce-scatter.2.cloned.1.call-start = ((), (), s32[]{:S(2)}) async-start(), calls=%async_computation.1 | async-start | bytes 368640 | tf_op jit(solution)/shard_map/reduce_scatter | solution.py:14
  7.2 26.1 %copy-start.1 = (f32[8,4608]{1,0:T(8,128)S(1)}, f32[8,4608]{1,0:T(8,128)}, u32[]{:S(2)}) copy-start(f32[8,4608]{1,0:T(8,128)} %param.7) | copy-start | bytes 442372
  7.9 43.6 %all-reduce.3.cloned.1.call-start = ((), (), s32[]{:S(2)}) async-start(), calls=%async_computation.2 | async-start | bytes 147456 | tf_op jit(solution)/shard_map/psum | solution.py:17
  33.2 42.7 %all-reduce.5.cloned.1.call-start = ((), (), s32[]{:S(2)}) async-start(), calls=%async_computation.3 | async-start | bytes 147456 | tf_op jit(solution)/shard_map/psum | solution.py:17
  51.5 39.0 %copy-start.2 = (f32[8,4608]{1,0:T(8,128)S(1)}, f32[8,4608]{1,0:T(8,128)}, u32[]{:S(2)}) copy-start(f32[8,4608]{1,0:T(8,128)} %param.6) | copy-start | bytes 442372
  51.5 39.0 %copy-start.3 = (f32[8,4608]{1,0:T(8,128)S(1)}, f32[8,4608]{1,0:T(8,128)}, u32[]{:S(2)}) copy-start(f32[8,4608]{1,0:T(8,128)} %param.5) | copy-start | bytes 442372
  75.9 14.6 %copy-start = (bf16[8,4608]{1,0:T(8,128)(2,1)S(1)}, bf16[8,4608]{1,0:T(8,128)(2,1)}, u32[]{:S(2)}) copy-start(bf16[8,4608]{1,0:T(8,128)(2,1)} %all-reduce.5.cloned.1.call-done) | copy-start | bytes 221188
Sparse Core Ops, SparseCore 0:
  10.2 22.9 reduce-scatter.1
  35.5 15.9 all-reduce.2
  53.7 22.1 all-reduce.4
